TPU v7x, 32 devices: a whole 2x2x4 slice. The times are simulated.
32 devices in a mesh: grp: 4 (over y, x), row: 8 (over z, core).
Axes of the slice: x: 2, y: 2, z: 4, core: 2. Of those that a mesh axis runs over, the one named last changes fastest.
Arguments:
- blocks: bfloat16 [32, 4, 10, 256, 256], P(('grp', 'row')), may hold values from 0 to 1
- columns: int32 [32, 4, 10], P(('grp', 'row')), may hold values from -1 to 31, as said below
- factor: bfloat16 [64, 8192], P(None, ('grp', 'row')), may hold values from 0 to 0.3, as said below
Outputs:
- updated: float32 [64, 8192], P(None, ('grp', 'row'))
Inputs may be any that keep to these rules, and one draw needn't show every extreme that they name: Tile row i lies in group g = i // 8. In block h of tile row i the live slots come first and name distinct tile columns of group h (h * 8 to h * 8 + 7), none above i; block g always names i itself; blocks h > g are empty; a block holds at most 10 live slots, and -1 marks an empty slot. `factor`: entries are nonnegative.
All inputs are finite; a program needn't handle non-finite values.
Results may differ from a plain program's by a relative error of at most 0.0003.
Values may be sent and summed in bfloat16 or wider, within the bound.
No kernel may reach another device: no remote copies, remote signals or barrier semaphores. Data moves between devices by JAX's collectives and lax.ppermute only.
A program may use at most 128 MiB of HBM per device.

v0:
```python
import jax
import jax.numpy as jnp
from jax import lax
from jax.sharding import PartitionSpec as P

floor_value = 1e-06


def sweep(current, products, gram):

    def update(column, current):
        weights = lax.dynamic_index_in_dim(gram, column, 1, keepdims=False)
        fitted = jnp.dot(weights, current, precision=lax.Precision.HIGHEST)
        target = lax.dynamic_index_in_dim(products, column, 0, keepdims=False)
        present = lax.dynamic_index_in_dim(current, column, 0, keepdims=False)
        diagonal = gram[column, column]
        fresh = jnp.maximum(present + (target - fitted) / diagonal, floor_value)
        return lax.dynamic_update_index_in_dim(current, fresh, column, 0)

    return lax.fori_loop(0, current.shape[0], update, current)


def choose_rows(group_cols, group_number, rows_grp):
    offsets = group_cols - group_number * rows_grp
    positions = lax.broadcasted_iota(jnp.int32, (group_cols.shape[0], rows_grp), 1)
    return (offsets[:, None] == positions) & (group_cols >= 0)[:, None]


def lower_work(group_tiles, group_cols, group_number, group_factor, rows_grp):
    rank_count, span = group_factor.shape
    tile_size = span // rows_grp
    stacked = group_factor.reshape(rank_count, rows_grp, tile_size)
    selected = choose_rows(group_cols, group_number, rows_grp)
    fetched = jnp.einsum(
        "sn,rnt->srt", selected.astype(jnp.bfloat16), stacked, preferred_element_type=jnp.float32
    ).astype(jnp.bfloat16)
    return jnp.einsum("srv,suv->ru", fetched, group_tiles, preferred_element_type=jnp.float32)


def per_device(blocks, columns, factor):
    tiles_dev = blocks[0]
    cols_dev = columns[0]
    rank_count, tile_size = factor.shape
    rows_grp = lax.axis_size("row")
    group_count = lax.axis_size("grp")
    span = rows_grp * tile_size
    gram = lax.psum(jnp.dot(factor, factor.T, preferred_element_type=jnp.float32), ("grp", "row"))
    group_factor = lax.all_gather(factor, "row", axis=1, tiled=True)
    my_group = lax.axis_index("grp")
    slot_count = cols_dev.shape[1]
    live = (cols_dev >= 0).astype(jnp.float32)
    mirror = jnp.einsum("ru,hsuv->hsrv", factor, tiles_dev, preferred_element_type=jnp.float32)
    mirror = mirror * live[:, :, None, None]
    arrived, arrived_cols = (
        lax.all_to_all(mirror, "grp", split_axis=0, concat_axis=0, tiled=True),
        lax.all_to_all(cols_dev, "grp", split_axis=0, concat_axis=0, tiled=True),
    )
    flat_cols = arrived_cols.reshape(group_count * slot_count)
    selected = choose_rows(flat_cols, my_group, rows_grp).astype(jnp.float32)
    flat_mirror = arrived.reshape(group_count * slot_count, rank_count, tile_size)
    spread = jnp.einsum("sn,srv->rnv", selected, flat_mirror, precision=lax.Precision.HIGHEST)
    mirror_sum = lax.psum_scatter(
        spread.reshape(rank_count, span), "row", scatter_dimension=1, tiled=True
    )
    lower_sum = jnp.zeros((rank_count, tile_size), jnp.float32)
    piece = lax.all_gather(group_factor, "grp", axis=1, tiled=True)
    begin_at = jnp.int32(0)
    for offset in range(piece.shape[1] // span):
        group_number = begin_at // span + offset
        group_tiles = lax.dynamic_index_in_dim(tiles_dev, group_number, 0, keepdims=False)
        group_cols = lax.dynamic_index_in_dim(cols_dev, group_number, 0, keepdims=False)
        block_cols = lax.dynamic_slice_in_dim(piece, offset * span, span, 1)
        lower_sum = lower_sum + lower_work(
            group_tiles, group_cols, group_number, block_cols, rows_grp
        )
    products = lower_sum + mirror_sum
    return sweep(factor.astype(jnp.float32), products, gram)


def solution(mesh):
    in_specs = (
        P(("grp", "row"), None, None, None, None),
        P(("grp", "row"), None, None),
        P(None, ("grp", "row")),
    )
    out_specs = P(None, ("grp", "row"))
    return jax.shard_map(
        per_device, mesh=mesh, in_specs=in_specs, out_specs=out_specs, check_vma=False
    )
```

profile of v0, /device:TPU:0, one launch (start us, length us, event | category | flops | bytes accessed | tf_op | source)
XLA Modules:
  0.0 246.8 jit_solution(16195418602525848965)
XLA Ops:
  7.4 5.2 %all-to-all-start.1 = ((s32[4,1,10]{2,1,0:T(1,128)}), s32[4,1,10]{2,1,0:T(1,128)S(1)}, u32[]{:S(2)}, u32[]{:S(2)}) async-start(s32[4,1,10]{2,1,0:T(1,128)} %bitcast.144), calls=%async_computation.1 | async-start | bytes 4096 | tf_op jit(solution)/shard_map/all_to_all | solution.py:56
  12.6 15.7 %all_gather.6 = bf16[64,2048]{1,0:T(8,128)(2,1)} all-gather(bf16[64,256]{1,0:T(8,128)(2,1)} %param.7), channel_id=1, replica_groups=mesh['grp'=4,'row'=8] {'row'}, dimensions={1}, use_global_device_ids=true | all-gather | bytes 294912 | tf_op jit(solution)/shard_map/all_gather | solution.py:48
  28.3 0.7 convert_bitcast_fusion
  29.0 5.1 %multiply_bitcast_fusion = f32[4,10,64,256]{3,2,1,0:T(8,128)} fusion(bf16[1,4,10,256,256]{4,3,2,1,0:T(8,128)(2,1)} %param.5, f32[4,10]{1,0:T(4,128)S(1)} %convert_bitcast_fusion, bf16[64,256]{1,0:T(8,128)(2,1)} %param.7), kind=kOutput, calls=%fused_computation.10 | convolution fusion | flops 336199680 | bytes 7897248 | tf_op jit(solution)/shard_map/ru,hsuv->hsrv/dot_general | solution.py:52
  34.1 4.4 %all-to-all-start = ((f32[4,10,64,256]{3,2,1,0:T(8,128)}), f32[4,10,64,256]{3,2,1,0:T(8,128)S(1)}, u32[]{:S(2)}, u32[]{:S(2)}) async-start(f32[4,10,64,256]{3,2,1,0:T(8,128)} %multiply_bitcast_fusion), calls=%async_computation | async-start | bytes 5242880 | tf_op jit(solution)/shard_map/all_to_all | solution.py:55
  38.6 71.8 %psum.7 = f32[64,64]{1,0:T(8,128)S(1)} all-reduce(f32[64,64]{1,0:T(8,128)S(1)} %fusion.75), channel_id=1, replica_groups=mesh['grp'=4,'row'=8] {'grp','row'}, use_global_device_ids=true, to_apply=%region_0.0 | all-reduce | flops 4096 | bytes 32768 | tf_op jit(solution)/shard_map/psum | solution.py:47
  110.8 1.3 fusion.74
  112.2 1.2 convolution_convert_fusion.3
  113.3 1.1 convolution_convert_fusion.2
  114.5 2.4 fusion.4
  116.9 1.0 copy.21
  117.9 2.0 fusion.20
  120.7 1.8 fusion.41
  122.5 1.8 fusion.38
  124.4 24.2 %reduce-scatter.2.cloned.1.call-done = f32[64,256]{1,0:T(8,128)} async-done(((f32[64,2048]{1,0:T(8,128)}), f32[64,256]{1,0:T(8,128)}) %reduce-scatter.2.cloned.1.call-update) | async-done | bytes 65552 | tf_op jit(solution)/shard_map/reduce_scatter | solution.py:62
  148.6 1.8 fusion.35
  150.4 88.3 %while.13 = (s32[]{:T(128)}, f32[64,256]{1,0:T(8,128)S(1)}, f32[64,256]{1,0:T(8,128)S(1)}, f32[64,64]{0,1:T(8,128)S(1)}, s32[]{:T(128)}, /*index=5*/s32[]{:T(128)}) while((s32[]{:T(128)}, f32[64,256]{1,0:T(8,128)S(1)}, f32[64,256]{1,0:T(8,128)S(1)}, f32[64,64]{0,1:T(8,128)S(1)}, s32[]{:T(128)}, /*index=5*/s32[]{:T(128)}) %tuple.42), condition=%wide.region_3.4_spmd, body=%wide.region_2.3_spmd.sunk | while | flops 197634 | bytes 77417 | solution.py:20
  150.6 0.6 dynamic_slice.138
  151.9 0.6 dynamic_slice.138
  153.3 0.6 dynamic_slice.138
  154.7 0.6 dynamic_slice.138
  156.1 0.6 dynamic_slice.138
  157.5 0.6 dynamic_slice.138
  158.8 0.6 dynamic_slice.138
  160.2 0.6 dynamic_slice.138
  161.6 0.6 dynamic_slice.138
  163.0 0.6 dynamic_slice.138
  164.4 0.6 dynamic_slice.138
  165.7 0.6 dynamic_slice.138
  167.1 0.6 dynamic_slice.138
  168.5 0.6 dynamic_slice.138
  238.7 0.6 copy-done
  (336 shorter events, 79.3 us)
Async XLA Ops:
  7.4 26.7 %all-to-all-start.1 = ((s32[4,1,10]{2,1,0:T(1,128)}), s32[4,1,10]{2,1,0:T(1,128)S(1)}, u32[]{:S(2)}, u32[]{:S(2)}) async-start(s32[4,1,10]{2,1,0:T(1,128)} %bitcast.144), calls=%async_computation.1 | async-start | bytes 4096 | tf_op jit(solution)/shard_map/all_to_all | solution.py:56
  12.6 98.2 %all-gather.2.cloned.1.call-start = ((), (), s32[]{:S(2)}) async-start(), calls=%async_computation.3 | async-start | bytes 1310720 | tf_op jit(solution)/shard_map/all_gather | solution.py:66
  34.0 4.4 %copy-start.1 = (bf16[64,256]{1,0:T(8,128)(2,1)S(1)}, bf16[64,256]{1,0:T(8,128)(2,1)}, u32[]{:S(2)}) copy-start(bf16[64,256]{1,0:T(8,128)(2,1)} %param.7) | copy-start | bytes 98308
  34.0 76.4 %copy-start.3 = (s32[1,4,10]{2,1,0:T(4,128)S(1)}, s32[1,4,10]{2,1,0:T(4,128)}, u32[]{:S(2)}) copy-start(s32[1,4,10]{2,1,0:T(4,128)} %param.6) | copy-start | bytes 484
  34.1 80.4 %all-to-all-start = ((f32[4,10,64,256]{3,2,1,0:T(8,128)}), f32[4,10,64,256]{3,2,1,0:T(8,128)S(1)}, u32[]{:S(2)}, u32[]{:S(2)}) async-start(f32[4,10,64,256]{3,2,1,0:T(8,128)} %multiply_bitcast_fusion), calls=%async_computation | async-start | bytes 5242880 | tf_op jit(solution)/shard_map/all_to_all | solution.py:55
  38.4 110.1 %reduce-scatter.2.cloned.1.call-start = ((), (), s32[]{:S(2)}) async-start(), calls=%async_computation.4 | async-start | bytes 589824 | tf_op jit(solution)/shard_map/reduce_scatter | solution.py:62
  117.8 2.9 %copy-start.2 = (bf16[10,64,256]{2,0,1:T(8,128)(2,1)S(1)}, bf16[10,64,256]{2,0,1:T(8,128)(2,1)}, u32[]{:S(2)}) copy-start(bf16[10,64,256]{2,0,1:T(8,128)(2,1)} %convolution_convert_fusion.2) | copy-start | bytes 983044
  238.7 0.6 copy-start
Sparse Core Ops, SparseCore 0:
  28.4 48.7 all-gather.1
Sparse Core Ops, SparseCore 1:
  117.9 30.6 reduce-scatter.1
where the time goes:
time: 248 us; the launch traced here: 247 us
  blocking collectives  87.5 us (35%)
  local copies, waits for them, and re-layouts  44.1 us (18%)
  other arithmetic  36.8 us (15%)
  matrix products  27.2 us (11%)
  waiting for transfers between devices  24.2 us (10%)
  between operations  15 us (6%)
  starting transfers between devices  9.57 us (4%)
    psum x1, blocking collectives, per_device(): lax.psum(jnp.dot(factor, factor.T, preferred_element_type=jnp.float32), (...  71.8 us
    dynamic_slice x64, local copies, waits for them, and re-layouts, update(): diagonal = gram[column, column]  37.4 us
    max x64, other arithmetic, update(): fresh = jnp.maximum(present + (target - fitted) / diagonal, floor_value)  36.1 us
    reduce_scatter x1, waiting for transfers between devices, per_device(): lax.psum_scatter(spread.reshape(rank_count, span), 'row', scatter_dimensi...  24.2 us
    all_gather x1, blocking collectives, per_device(): group_factor = lax.all_gather(factor, 'row', axis=1, tiled=True)  15.7 us
    dot_general x64, matrix products, update(): fitted = jnp.dot(weights, current, precision=lax.Precision.HIGHEST)  9.16 us
    dot_general x4, matrix products, lower_work(): jnp.einsum('srv,suv->ru', fetched, group_tiles, preferred_element_type=jn...  7.5 us
    all_to_all x1, starting transfers between devices, per_device(): lax.all_to_all(cols_dev, 'grp', split_axis=0, concat_axis=0, tiled=True)  5.19 us
  transfers between devices with their start and end apart: 4, of which 1 were waited for; matrix products, arithmetic and copies ran while one was open for 7% of the time, Pallas kernels for 0%

commit v1 on v0

--- a/solution.py
+++ b/solution.py
@@ -44,7 +44,9 @@
     rows_grp = lax.axis_size("row")
     group_count = lax.axis_size("grp")
     span = rows_grp * tile_size
-    gram = lax.psum(jnp.dot(factor, factor.T, preferred_element_type=jnp.float32), ("grp", "row"))
+    gram = jnp.dot(factor, factor.T, preferred_element_type=jnp.float32)
+    for over in ("row", "grp"):
+        gram = lax.psum(gram, over)
     group_factor = lax.all_gather(factor, "row", axis=1, tiled=True)
     my_group = lax.axis_index("grp")
     slot_count = cols_dev.shape[1]

time: 248 us -> 229 us (0.923)
  blocking collectives: 87.5 us -> 63.5 us
  other arithmetic: 36.8 us -> 40.6 us
    psum x1 -> x2, blocking collectives: 71.8 us -> 47.7 us  [per_device(): gram = lax.psum(gram, over)]
    max x64, other arithmetic: 36.1 us -> 39.8 us  [update(): fresh = jnp.maximum(present + (target - fitted) / diagonal, floor_value)]
where the time goes in v1:
time: 229 us; the launch traced here: 228 us
  blocking collectives  63.5 us (28%)
  local copies, waits for them, and re-layouts  45.1 us (20%)
  other arithmetic  40.6 us (18%)
  matrix products  27.2 us (12%)
  waiting for transfers between devices  24.8 us (11%)
  between operations  15 us (7%)
  starting transfers between devices  9.57 us (4%)
  loops' own time  2.29 us (1%)
    psum x2, blocking collectives, per_device(): gram = lax.psum(gram, over)  47.7 us
    max x64, other arithmetic, update(): fresh = jnp.maximum(present + (target - fitted) / diagonal, floor_value)  39.8 us
    dynamic_slice x64, local copies, waits for them, and re-layouts, update(): diagonal = gram[column, column]  38.4 us
    reduce_scatter x1, waiting for transfers between devices, per_device(): lax.psum_scatter(spread.reshape(rank_count, span), 'row', scatter_dimensi...  24.8 us
    all_gather x1, blocking collectives, per_device(): group_factor = lax.all_gather(factor, 'row', axis=1, tiled=True)  15.7 us
    dot_general x64, matrix products, update(): fitted = jnp.dot(weights, current, precision=lax.Precision.HIGHEST)  9.16 us
    dot_general x4, matrix products, lower_work(): jnp.einsum('srv,suv->ru', fetched, group_tiles, preferred_element_type=jn...  7.48 us
    all_to_all x1, starting transfers between devices, per_device(): lax.all_to_all(cols_dev, 'grp', split_axis=0, concat_axis=0, tiled=True)  5.19 us
  transfers between devices with their start and end apart: 4, of which 1 were waited for; matrix products, arithmetic and copies ran while one was open for 7% of the time, Pallas kernels for 0%

profile of v1, /device:TPU:0, one launch (start us, length us, event | category | flops | bytes accessed | tf_op | source)
XLA Modules:
  0.0 228.1 jit_solution(4863688492358381266)
XLA Ops:
  7.4 5.2 %all-to-all-start.1 = ((s32[4,1,10]{2,1,0:T(1,128)}), s32[4,1,10]{2,1,0:T(1,128)S(1)}, u32[]{:S(2)}, u32[]{:S(2)}) async-start(s32[4,1,10]{2,1,0:T(1,128)} %bitcast.144), calls=%async_computation.1 | async-start | bytes 4096 | tf_op jit(solution)/shard_map/all_to_all | solution.py:58
  12.6 15.7 %all_gather.6 = bf16[64,2048]{1,0:T(8,128)(2,1)} all-gather(bf16[64,256]{1,0:T(8,128)(2,1)} %param.7), channel_id=1, replica_groups=mesh['grp'=4,'row'=8] {'row'}, dimensions={1}, use_global_device_ids=true | all-gather | bytes 294912 | tf_op jit(solution)/shard_map/all_gather | solution.py:50
  28.3 0.7 convert_bitcast_fusion
  29.0 5.0 %multiply_bitcast_fusion = f32[4,10,64,256]{3,2,1,0:T(8,128)} fusion(bf16[1,4,10,256,256]{4,3,2,1,0:T(8,128)(2,1)} %param.5, f32[4,10]{1,0:T(4,128)S(1)} %convert_bitcast_fusion, bf16[64,256]{1,0:T(8,128)(2,1)} %param.7), kind=kOutput, calls=%fused_computation.10 | convolution fusion | flops 336199680 | bytes 7897248 | tf_op jit(solution)/shard_map/ru,hsuv->hsrv/dot_general | solution.py:54
  34.0 4.4 %all-to-all-start = ((f32[4,10,64,256]{3,2,1,0:T(8,128)}), f32[4,10,64,256]{3,2,1,0:T(8,128)S(1)}, u32[]{:S(2)}, u32[]{:S(2)}) async-start(f32[4,10,64,256]{3,2,1,0:T(8,128)} %multiply_bitcast_fusion), calls=%async_computation | async-start | bytes 5242880 | tf_op jit(solution)/shard_map/all_to_all | solution.py:57
  38.6 28.8 %psum.14 = f32[64,64]{1,0:T(8,128)S(1)} all-reduce(f32[64,64]{1,0:T(8,128)S(1)} %fusion.75), channel_id=1, replica_groups=mesh['grp'=4,'row'=8] {'row'}, use_global_device_ids=true, to_apply=%region_0.0 | all-reduce | flops 4096 | bytes 32768 | tf_op jit(solution)/shard_map/psum | solution.py:49
  67.4 18.9 %psum.15 = f32[64,64]{1,0:T(8,128)S(1)} all-reduce(f32[64,64]{1,0:T(8,128)S(1)} %psum.14), channel_id=1, replica_groups=mesh['grp'=4,'row'=8] {'grp'}, use_global_device_ids=true, to_apply=%region_1.0 | all-reduce | flops 4096 | bytes 32768 | tf_op jit(solution)/shard_map/psum | solution.py:49
  86.6 1.3 fusion.74
  88.1 1.2 convolution_convert_fusion.3
  89.2 1.1 convolution_convert_fusion.2
  90.4 2.4 %fusion.4 = f32[64,256,8]{1,2,0:T(8,128)S(1)} fusion(f32[40,64,256]{2,1,0:T(8,128)S(1)} %bitcast.129, s32[40]{0:T(128)S(1)} %sub.63, pred[40]{0:T(512)(128)(4,1)S(1)} %ge.72), kind=kOutput, calls=%fused_computation.8 | convolution fusion | flops 62915200 | bytes 3145928 | tf_op jit(solution)/shard_map/sn,srv->rnv/dot_general | solution.py:63
  92.8 1.0 copy.21
  93.8 2.0 fusion.20
  96.6 1.8 fusion.41
  98.4 1.8 fusion.38
  100.3 24.8 %reduce-scatter.2.cloned.1.call-done = f32[64,256]{1,0:T(8,128)} async-done(((f32[64,2048]{1,0:T(8,128)}), f32[64,256]{1,0:T(8,128)}) %reduce-scatter.2.cloned.1.call-update) | async-done | bytes 65552 | tf_op jit(solution)/shard_map/reduce_scatter | solution.py:64
  125.1 1.8 fusion.35
  126.9 93.1 %while.13 = (s32[]{:T(128)}, f32[64,256]{1,0:T(8,128)S(1)}, f32[64,256]{1,0:T(8,128)S(1)}, f32[64,64]{0,1:T(8,128)S(1)}, s32[]{:T(128)}, /*index=5*/s32[]{:T(128)}) while((s32[]{:T(128)}, f32[64,256]{1,0:T(8,128)S(1)}, f32[64,256]{1,0:T(8,128)S(1)}, f32[64,64]{0,1:T(8,128)S(1)}, s32[]{:T(128)}, /*index=5*/s32[]{:T(128)}) %tuple.42), condition=%wide.region_4.5_spmd, body=%wide.region_3.4_spmd.sunk | while | flops 197634 | bytes 77417 | solution.py:20
  127.7 0.6 fusion.88
  129.1 0.6 fusion.88
  130.6 0.6 fusion.88
  136.4 0.6 fusion.88
  137.8 0.6 fusion.88
  139.3 0.6 fusion.88
  140.7 0.6 fusion.88
  145.1 0.6 fusion.88
  146.6 0.6 fusion.88
  148.0 0.6 fusion.88
  149.5 0.6 fusion.88
  155.3 0.6 fusion.88
  156.7 0.6 fusion.88
  158.2 0.6 fusion.88
  (337 shorter events, 84.1 us)
Async XLA Ops:
  7.4 26.7 %all-to-all-start.1 = ((s32[4,1,10]{2,1,0:T(1,128)}), s32[4,1,10]{2,1,0:T(1,128)S(1)}, u32[]{:S(2)}, u32[]{:S(2)}) async-start(s32[4,1,10]{2,1,0:T(1,128)} %bitcast.144), calls=%async_computation.1 | async-start | bytes 4096 | tf_op jit(solution)/shard_map/all_to_all | solution.py:58
  12.6 74.1 %all-gather.2.cloned.1.call-start = ((), (), s32[]{:S(2)}) async-start(), calls=%async_computation.3 | async-start | bytes 1310720 | tf_op jit(solution)/shard_map/all_gather | solution.py:68
  34.0 4.4 %copy-start.1 = (bf16[64,256]{1,0:T(8,128)(2,1)S(1)}, bf16[64,256]{1,0:T(8,128)(2,1)}, u32[]{:S(2)}) copy-start(bf16[64,256]{1,0:T(8,128)(2,1)} %param.7) | copy-start | bytes 98308
  34.0 52.4 %copy-start.3 = (s32[1,4,10]{2,1,0:T(4,128)S(1)}, s32[1,4,10]{2,1,0:T(4,128)}, u32[]{:S(2)}) copy-start(s32[1,4,10]{2,1,0:T(4,128)} %param.6) | copy-start | bytes 484
  34.0 56.3 %all-to-all-start = ((f32[4,10,64,256]{3,2,1,0:T(8,128)}), f32[4,10,64,256]{3,2,1,0:T(8,128)S(1)}, u32[]{:S(2)}, u32[]{:S(2)}) async-start(f32[4,10,64,256]{3,2,1,0:T(8,128)} %multiply_bitcast_fusion), calls=%async_computation | async-start | bytes 5242880 | tf_op jit(solution)/shard_map/all_to_all | solution.py:57
  38.4 86.7 %reduce-scatter.2.cloned.1.call-start = ((), (), s32[]{:S(2)}) async-start(), calls=%async_computation.4 | async-start | bytes 589824 | tf_op jit(solution)/shard_map/reduce_scatter | solution.py:64
  93.7 2.9 %copy-start.2 = (bf16[10,64,256]{2,0,1:T(8,128)(2,1)S(1)}, bf16[10,64,256]{2,0,1:T(8,128)(2,1)}, u32[]{:S(2)}) copy-start(bf16[10,64,256]{2,0,1:T(8,128)(2,1)} %convolution_convert_fusion.2) | copy-start | bytes 983044
  220.0 0.6 copy-start
Sparse Core Ops, SparseCore 0:
  28.4 48.7 all-gather.1
Sparse Core Ops, SparseCore 1:
  93.8 31.2 reduce-scatter.1
